TPU v7x, 512 devices: a 4x2x32 block of a 4x8x32 slice. The times are simulated.
512 devices in a mesh: groups: 2 (over y), tp: 8 (over x, core), sp: 32 (over z).
Axes of the slice: x: 4, y: 2, z: 32, core: 2. Of those that a mesh axis runs over, the one named last changes fastest.
The devices are a block of a 4x8x32 slice.
Arguments:
- query_rows: bfloat16 [4, 2048, 4096], P('groups', ('sp', 'tp')), parts along dimension 0, may hold values from -100 to 100
- key_rows: bfloat16 [4, 2048, 4096], P('groups', ('sp', 'tp')), parts along dimension 0, may hold values from -4 to 4
- value_rows: bfloat16 [4, 2048, 4096], P('groups', ('sp', 'tp')), parts along dimension 0, may hold values from -6 to 6
- residual: bfloat16 [4, 2048, 2560], P('groups', 'sp', 'tp'), parts along dimension 0, may hold values from -100 to 100
- modulation: float32 [4, 2560], P(None, 'tp'), may hold values from -3 to 3
- out_weight: bfloat16 [2560, 4096], P('tp', 'sp'), may hold values from -0.375 to 0.375
- up_weight: bfloat16 [2560, 7168], P('sp', 'tp'), may hold values from -0.125 to 0.125
- down_weight: bfloat16 [2560, 7168], P('sp', 'tp'), may hold values from -0.0625 to 0.0625
Outputs:
- block_out: bfloat16 [4, 2048, 2560], P('groups', 'sp', 'tp'), parts along dimension 0
There are 2 independent parts, one for each index of `groups`. A program takes and returns all parts, laid end to end along the dimension named above; an argument that names none is the same for every part. Nothing has to cross between parts.
All inputs are finite; a program needn't handle non-finite values.
Results may differ from a plain program's by a relative error of at most 0.0044.
Values may be sent and summed in bfloat16 or wider, within the bound.
A program may use at most 64 MiB of HBM per device.

v0:
```python
import math

import jax
import jax.numpy as jnp
from jax import lax
from jax.sharding import PartitionSpec as P

D = 2560
HEAD_FEATURES = 128


def in_one_piece(arrays, axis, split_dim, concat_dim, along):
    widths = [a.shape[along] for a in arrays]
    both = jnp.concatenate(arrays, axis=along)
    filled = lax.all_to_all(both, axis, split_axis=split_dim, concat_axis=concat_dim, tiled=True)
    return tuple(jnp.split(filled, [sum(widths[:k]) for k in range(1, len(widths))], axis=along))


def side_by_side(arrays, axis, dim, along):
    both = jnp.concatenate(arrays, axis=along)
    filled, at, outs = (lax.all_gather(both, axis, axis=dim, tiled=True), 0, [])
    for a in arrays:
        outs.append(lax.slice_in_dim(filled, at, at + a.shape[along], axis=along))
        at += a.shape[along]
    return tuple(outs)


def sent_to_all(array, axis):
    copies = jnp.broadcast_to(array, (lax.axis_size(axis), *array.shape))
    return lax.all_to_all(copies, axis, split_axis=0, concat_axis=0, tiled=True)


def joined_along(parts, dim):
    dims = list(parts.shape[1:])
    dims[dim] *= parts.shape[0]
    return jnp.moveaxis(parts, 0, dim).reshape(dims)


def gathered_copies(array, axis, dim):
    parts = sent_to_all(array, axis)
    return joined_along(parts, dim)


def taken_together(array, axis):
    everything = sent_to_all(array, axis)
    return jnp.sum(everything, axis=0)


def packed_total(arrays, axis):
    flat, at, outs = (jnp.concatenate([a.reshape(-1) for a in arrays]), 0, [])
    so_far = taken_together(flat, axis)
    for a in arrays:
        outs.append(so_far[at : at + a.size].reshape(a.shape))
        at += a.size
    return tuple(outs)


def in_blocks(array, dim, peers):
    before, after = (array.shape[:dim], array.shape[dim + 1 :])
    return jnp.moveaxis(array.reshape(*before, peers, -1, *after), dim, 0)


def sent_and_summed(array, axis, dim):
    peers = lax.axis_size(axis)
    parts = lax.all_to_all(in_blocks(array, dim, peers), axis, 0, 0, tiled=True)
    return jnp.sum(parts.astype(jnp.float32), axis=0)


def contract_last(left, right):
    return lax.dot_general(
        left, right, (((1,), (1,)), ((), ())), preferred_element_type=jnp.float32
    )


def attend(query_part, key_part, value_part):
    query_heads, key_heads, value_heads = in_one_piece(
        (query_part, key_part, value_part), "sp", 2, 1, 0
    )
    batches, query_count, local_width = query_heads.shape
    local_heads = local_width // HEAD_FEATURES
    grouped = query_heads.reshape(batches, query_count, local_heads, HEAD_FEATURES)
    score_scale = 1.0 / math.sqrt(HEAD_FEATURES)

    def absorb_block(running, blocks):
        block_keys, block_values = blocks
        highest, row_total, weighted_values = running
        attention_logits = (
            jnp.einsum("bqhd,bkhd->bqhk", grouped, block_keys, preferred_element_type=jnp.float32)
            * score_scale
        )
        raised = jnp.maximum(highest, jnp.max(attention_logits, axis=-1))
        damping = jnp.exp(highest - raised)
        exponent = jnp.exp(attention_logits - raised[..., None])
        row_total = row_total * damping + jnp.sum(exponent, axis=-1)
        weighted_values = weighted_values * damping[..., None] + jnp.einsum(
            "bqhk,bkhd->bqhd",
            exponent.astype(jnp.bfloat16),
            block_values,
            preferred_element_type=jnp.float32,
        )
        return (raised, row_total, weighted_values)

    def scan_step(running, blocks):
        return (absorb_block(running, blocks), None)

    starting = (
        jnp.full((batches, query_count, local_heads), -jnp.inf, jnp.float32),
        jnp.zeros((batches, query_count, local_heads), jnp.float32),
        jnp.zeros((batches, query_count, local_heads, HEAD_FEATURES), jnp.float32),
    )
    running = starting
    key_section, value_section = side_by_side((key_heads, value_heads), "tp", 1, 0)
    key_count = key_section.shape[1]
    shaped_keys = key_section.reshape(batches, key_count, local_heads, HEAD_FEATURES)
    shaped_values = value_section.reshape(batches, key_count, local_heads, HEAD_FEATURES)
    block_count = key_count // 512
    key_blocks = jnp.moveaxis(
        shaped_keys.reshape(batches, block_count, 512, local_heads, HEAD_FEATURES), 1, 0
    )
    value_blocks = jnp.moveaxis(
        shaped_values.reshape(batches, block_count, 512, local_heads, HEAD_FEATURES), 1, 0
    )
    running, unused = lax.scan(scan_step, running, (key_blocks, value_blocks))
    highest, row_total, weighted_values = running
    normalized = (weighted_values / row_total[..., None]).astype(jnp.bfloat16)
    ordered = normalized.reshape(batches, query_count, local_width)
    return lax.all_to_all(ordered, "sp", split_axis=1, concat_axis=2, tiled=True)


def body(
    query_rows, key_rows, value_rows, residual, modulation, out_weight, up_weight, down_weight
):
    attended = attend(query_rows, key_rows, value_rows)
    stripes = gathered_copies(attended, "tp", 1)
    batches, rows_block, inner_width = stripes.shape
    row_count = batches * rows_block
    flat_rows = stripes.reshape(row_count, inner_width)
    local_width = out_weight.shape[0]
    columns = flat_rows
    projected = contract_last(columns, lax.all_gather(out_weight, "sp", axis=1, tiled=True))
    mixed_rows = (
        residual.reshape(row_count, local_width).astype(jnp.float32) + modulation[0] * projected
    )
    first_sum, second_sum = packed_total(
        (jnp.sum(mixed_rows, axis=1), jnp.sum(mixed_rows * mixed_rows, axis=1)), "tp"
    )
    row_mean = first_sum / D
    spread = second_sum / D - row_mean * row_mean
    normed = (
        (mixed_rows - row_mean[:, None])
        * lax.rsqrt(spread[:, None] + 1e-06)
        * (1.0 + modulation[2])
        + modulation[1]
    ).astype(jnp.bfloat16)
    gathered = gathered_copies(normed, "tp", 1)
    columns = gathered
    hidden = jnp.dot(
        columns,
        lax.all_gather(up_weight, "sp", axis=0, tiled=True),
        preferred_element_type=jnp.float32,
    )
    active = jax.nn.gelu(hidden, approximate=True).astype(jnp.bfloat16)
    partial_out = contract_last(active, lax.all_gather(down_weight, "sp", axis=0, tiled=True))
    summed = sent_and_summed(partial_out.astype(jnp.bfloat16), "tp", 1)
    result = (mixed_rows + modulation[3] * summed).astype(jnp.bfloat16)
    return result.reshape(batches, rows_block, local_width)


def solution(mesh):
    in_specs = (
        P("groups", ("sp", "tp"), None),
        P("groups", ("sp", "tp"), None),
        P("groups", ("sp", "tp"), None),
        P("groups", "sp", "tp"),
        P(None, "tp"),
        P("tp", "sp"),
        P("sp", "tp"),
        P("sp", "tp"),
    )
    out_specs = P("groups", "sp", "tp")
    return jax.shard_map(body, mesh=mesh, in_specs=in_specs, out_specs=out_specs, check_vma=False)
```

profile of v0, /device:TPU:33, one launch (start us, length us, event | category | flops | bytes accessed | tf_op | source)
XLA Modules:
  0.0 618.6 jit_solution(4592646324095410421)
XLA Ops:
  6.5 0.0 all-gather.5.cloned.1.call-start
  6.6 1.1 pad_maximum_fusion
  7.6 7.2 %copy.59 = bf16[6,8,4096]{1,0,2:T(8,128)(2,1)} copy(bf16[6,8,4096]{2,1,0:T(8,128)(2,1)S(1)} %pad_maximum_fusion) | data formatting | bytes 786432 | tf_op jit(solution)/shard_map/concatenate | solution.py:14
  14.8 9.2 %reshape.73 = bf16[32,2,3072]{2,1,0:T(2,128)(2,1)S(1)} reshape(bf16[4096,6,8]{2,1,0:T(8,128)(2,1)} %bitcast.97) | data formatting | bytes 786432
  24.0 97.4 %all_to_all.54 = bf16[32,2,3072]{2,1,0:T(2,128)(2,1)S(1)} all-to-all(bf16[32,2,3072]{2,1,0:T(2,128)(2,1)S(1)} %reshape.73), channel_id=1, replica_groups=mesh['groups'=2,'tp'=8,'sp'=32] {'sp'}, dimensions={0} | all-to-all | bytes 786432 | tf_op jit(solution)/shard_map/all_to_all | solution.py:15
  121.3 8.7 %reshape.74 = bf16[4096,6,8]{2,1,0:T(8,128)(2,1)} reshape(bf16[32,2,3072]{2,1,0:T(2,128)(2,1)S(1)} %all_to_all.54) | data formatting | bytes 786432
  130.0 7.4 %copy.60 = bf16[6,8,32,128]{3,1,2,0:T(8,128)(2,1)S(1)} copy(bf16[6,8,32,128]{1,0,3,2:T(8,128)(2,1)} %bitcast.98) | data formatting | bytes 786432 | tf_op jit(solution)/shard_map/all_to_all | solution.py:15
  137.5 0.7 pad_maximum_fusion.1
  138.2 0.1 all-gather.5.cloned.1.call-update
  138.2 0.1 all-gather.7.cloned.1.call-start
  138.3 0.7 all-gather.7.cloned.1.call-update
  139.1 0.1 all-gather.11.cloned.1.call-start
  139.1 0.7 all-gather.11.cloned.1.call-update
  139.9 0.1 all-gather.9.cloned.1.call-start
  139.9 0.6 all-gather.9.cloned.1.call-update
  140.5 24.1 %all-gather.5.cloned.1.call-done = bf16[4,2048,128]{2,1,0:T(8,128)(2,1)} async-done(((bf16[4,256,128]{2,1,0:T(8,128)(2,1)}), bf16[4,2048,128]{2,1,0:T(8,128)(2,1)}) %all-gather.5.cloned.1.call-update) | async-done | bytes 2097168 | tf_op jit(solution)/shard_map/all_gather | solution.py:21
  164.6 1.7 fusion.36
  166.3 3.9 while.15
  166.3 0.3 fusion.52
  166.7 0.4 fusion.55
  167.1 0.2 fusion.54
  167.3 0.3 fusion.52
  167.6 0.4 fusion.55
  168.1 0.2 fusion.54
  168.3 0.3 fusion.52
  168.6 0.4 fusion.55
  169.0 0.2 fusion.54
  169.2 0.3 fusion.52
  169.6 0.4 fusion.55
  170.0 0.2 fusion.54
  170.2 0.0 copy-start
  170.2 0.0 copy-start.1
  170.2 0.1 copy.64
  170.4 0.1 copy.63
  170.5 0.3 fusion.29
  170.9 53.5 %all_to_all.55 = bf16[2,256,128]{2,0,1:T(2,128)(2,1)S(1)} all-to-all(bf16[2,256,128]{2,0,1:T(2,128)(2,1)S(1)} %fusion.29), channel_id=1, replica_groups=mesh['groups'=2,'tp'=8,'sp'=32] {'sp'}, dimensions={1} | all-to-all | bytes 262144 | tf_op jit(solution)/shard_map/all_to_all | solution.py:127
  224.4 1.1 broadcast_in_dim.27
  225.5 6.0 all-to-all-start.2
  231.5 0.0 copy-done
  231.5 0.1 copy.67
  231.7 0.0 copy-done.1
  231.7 14.9 %all-to-all-done.2 = bf16[8,2,8,4096]{3,2,1,0:T(8,128)(2,1)S(1)} async-done(((bf16[8,2,8,4096]{3,2,1,0:T(8,128)(2,1)}), bf16[8,2,8,4096]{3,2,1,0:T(8,128)(2,1)S(1)}, u32[]{:S(2)}, u32[]{:S(2)}) %all-to-all-start.2) | async-done | bytes 1048608 | tf_op jit(solution)/shard_map/all_to_all | solution.py:30
  246.6 0.1 copy.66
  246.7 47.1 %all-gather.7.cloned.1.call-done = bf16[320,4096]{1,0:T(8,128)(2,1)} async-done(((bf16[320,128]{1,0:T(8,128)(2,1)}), bf16[320,4096]{1,0:T(8,128)(2,1)}) %all-gather.7.cloned.1.call-update) | async-done | bytes 2621456 | tf_op jit(solution)/shard_map/all_gather | solution.py:140
  293.8 2.6 fusion.34
  296.4 33.6 %all_to_all.56 = f32[8,1,256]{2,1,0:T(1,128)S(1)} all-to-all(f32[8,1,256]{2,1,0:T(1,128)S(1)} %broadcast_in_dim.28), channel_id=1, replica_groups=mesh['groups'=2,'tp'=8,'sp'=32] {'tp'}, dimensions={0} | all-to-all | bytes 16384 | tf_op jit(solution)/shard_map/all_to_all | solution.py:30
  330.1 0.2 add_convert_fusion.1
  330.3 0.9 broadcast_in_dim.29
  331.2 4.2 all-to-all-start.4
  335.4 99.1 %all-gather.11.cloned.1.call-done = bf16[2560,896]{1,0:T(8,128)(2,1)} async-done(((bf16[80,896]{1,0:T(8,128)(2,1)}), bf16[2560,896]{1,0:T(8,128)(2,1)}) %all-gather.11.cloned.1.call-update) | async-done | bytes 4587536 | tf_op jit(solution)/shard_map/all_gather | solution.py:163
  434.5 134.8 %all-gather.9.cloned.1.call-done = bf16[2560,896]{1,0:T(8,128)(2,1)} async-done(((bf16[80,896]{1,0:T(8,128)(2,1)}), bf16[2560,896]{1,0:T(8,128)(2,1)}) %all-gather.9.cloned.1.call-update) | async-done | bytes 4587536 | tf_op jit(solution)/shard_map/all_gather | solution.py:159
  569.3 0.0 all-to-all-done.4
  569.3 6.0 convolution_convert_fusion
  575.3 0.3 copy.69
  575.7 35.5 %all_to_all.57 = bf16[8,128,320]{1,2,0:T(8,128)(2,1)S(1)} all-to-all(bf16[8,128,320]{1,2,0:T(8,128)(2,1)S(1)} %bitcast.103), channel_id=1, replica_groups=mesh['groups'=2,'tp'=8,'sp'=32] {'tp'}, dimensions={0} | all-to-all | bytes 1310720 | tf_op jit(solution)/shard_map/all_to_all | solution.py:65
  611.1 0.1 convert_reduce_fusion
  611.2 0.1 add_convert_fusion
  611.3 0.8 copy.70
  (23 shorter events, 0.3 us)
Async XLA Ops:
  6.5 158.1 %all-gather.5.cloned.1.call-start = ((), (), s32[]{:S(2)}) async-start(), calls=%async_computation.6 | async-start | bytes 2359296 | tf_op jit(solution)/shard_map/all_gather | solution.py:21
  138.2 155.6 %all-gather.7.cloned.1.call-start = ((), (), s32[]{:S(2)}) async-start(), calls=%async_computation.7 | async-start | bytes 2703360 | tf_op jit(solution)/shard_map/all_gather | solution.py:140
  139.1 295.4 %all-gather.11.cloned.1.call-start = ((), (), s32[]{:S(2)}) async-start(), calls=%async_computation.9 | async-start | bytes 4730880 | tf_op jit(solution)/shard_map/all_gather | solution.py:163
  139.9 429.4 %all-gather.9.cloned.1.call-start = ((), (), s32[]{:S(2)}) async-start(), calls=%async_computation.8 | async-start | bytes 4730880 | tf_op jit(solution)/shard_map/all_gather | solution.py:159
  170.2 61.3 %copy-start = (bf16[2,64,320]{2,1,0:T(8,128)(2,1)S(1)}, bf16[2,64,320]{2,1,0:T(8,128)(2,1)}, u32[]{:S(2)}) copy-start(bf16[2,64,320]{2,1,0:T(8,128)(2,1)} %param.13) | copy-start | bytes 245764
  170.2 61.4 %copy-start.1 = (f32[4,320]{1,0:T(4,128)S(1)}, f32[4,320]{1,0:T(4,128)}, u32[]{:S(2)}) copy-start(f32[4,320]{1,0:T(4,128)} %param.14) | copy-start | bytes 15364
  225.5 21.0 %all-to-all-start.2 = ((bf16[8,2,8,4096]{3,2,1,0:T(8,128)(2,1)}), bf16[8,2,8,4096]{3,2,1,0:T(8,128)(2,1)S(1)}, u32[]{:S(2)}, u32[]{:S(2)}) async-start(bf16[8,2,8,4096]{3,2,1,0:T(8,128)(2,1)} %broadcast_in_dim.27), calls=%async_computation.2 | async-start | bytes 2097152 | tf_op jit(solution)/shard_map/all_to_all | solution.py:30
  331.2 238.1 %all-to-all-start.4 = ((bf16[8,128,320]{1,2,0:T(8,128)(2,1)}), bf16[8,128,320]{1,2,0:T(8,128)(2,1)S(1)}, u32[]{:S(2)}, u32[]{:S(2)}) async-start(bf16[8,128,320]{1,2,0:T(8,128)(2,1)} %broadcast_in_dim.29), calls=%async_computation.4 | async-start | bytes 1310720 | tf_op jit(solution)/shard_map/all_to_all | solution.py:30
Sparse Core Ops, SparseCore 0:
  138.4 26.1 all-gather.4
  166.6 127.1 all-gather.6
  295.9 138.4 all-gather.10
  436.4 132.8 all-gather.8
where the time goes:
time: 619 us
  waiting for transfers between devices  322 us (52%)
  blocking collectives  220 us (36%)
  local copies, waits for them, and re-layouts  37.8 us (6%)
  between operations  13.3 us (2%)
  matrix products  11.6 us (2%)
  starting transfers between devices  10.3 us (2%)
    all_gather x1, waiting for transfers between devices, body(): lax.all_gather(up_weight, 'sp', axis=0, tiled=True)  135 us
    all_gather x1, waiting for transfers between devices, body(): lax.all_gather(down_weight, 'sp', axis=0, tiled=True)  99.1 us
    all_to_all x1, blocking collectives, in_one_piece(): lax.all_to_all(both, axis, split_axis=split_dim, concat_axis=concat_dim,...  97.4 us
    all_to_all x1, blocking collectives, attend(): lax.all_to_all(ordered, 'sp', split_axis=1, concat_axis=2, tiled=True)  53.5 us
    all_gather x1, waiting for transfers between devices, body(): lax.all_gather(out_weight, 'sp', axis=1, tiled=True)  47.1 us
    all_to_all x1, blocking collectives, sent_and_summed(): parts = lax.all_to_all(in_blocks(array, dim, peers), axis, 0, 0, tiled=True)  35.5 us
    all_to_all x1, blocking collectives, sent_to_all(): return lax.all_to_all(copies, axis, split_axis=0, concat_axis=0, tiled=True)  33.6 us
    all_gather x1, waiting for transfers between devices, side_by_side(): filled, at, outs = (lax.all_gather(both, axis, axis=dim, tiled=True), 0, [])  24.1 us
  transfers between devices with their start and end apart: 6, of which 5 were waited for; matrix products, arithmetic and copies ran while one was open for 2% of the time, Pallas kernels for 0%

commit v1 on v0

v1 whole, which is shorter than its diff:
```python
import functools
import math

import jax
import jax.numpy as jnp
from jax import lax
from jax.experimental import pallas as pl
from jax.experimental.pallas import tpu as pltpu
from jax.sharding import PartitionSpec as P

MESH = pl.DeviceIdType.MESH
F32 = jnp.float32
BF16 = jnp.bfloat16


def dot_last(a, b):
    return lax.dot_general(a, b, (((1,), (1,)), ((), ())), preferred_element_type=F32)


def dot(a, b):
    return jnp.dot(a, b, preferred_element_type=F32)


def kernel(
    sp, tp, q_hbm, k_hbm, v_hbm, res_ref, mod_ref, wo_hbm, up_hbm, dn_hbm, out_ref,
    qkv, qkvr, kvo, qp, kp, vp, scores, att, att_all, wo_full, w2, mixed, stats, normed_all,
    active, part_send, part_recv,
    local_sem, ring_recv, ring_send, pair_sem, far_sem, a2a_sem, kv_sem, back_sem, gat_sem, gnm_sem, st_sem, rs_sem,
):
    heads, feats = sp, qkvr.shape[-1]
    nx = tp // 2
    g, t, z = lax.axis_index("groups"), lax.axis_index("tp"), lax.axis_index("sp")
    x, c = t // 2, t % 2
    par = g % 2
    xr, xl, xo = (x + 1) % nx, (x + nx - 1) % nx, (x + 2) % nx
    zr, zl = (z + 1) % sp, (z + sp - 1) % sp
    sib = t + 1 - 2 * c
    pending = []

    def remote(src, dst, send, recv, dev):
        return pltpu.make_async_remote_copy(
            src_ref=src, dst_ref=dst, send_sem=send, recv_sem=recv, device_id=dev, device_id_type=MESH
        )

    def send(src, dst, s, r, dev):
        d = remote(src, dst, s, r, dev)
        d.start()
        pending.append(d)

    shard = up_hbm.shape[0]

    def w2rows(a, o):
        return w2.at[a, pl.ds(pl.multiple_of(o * shard, 16), shard), :]

    locals_w = [
        pltpu.make_async_copy(wo_hbm, wo_full.at[z], local_sem.at[0]),
        pltpu.make_async_copy(up_hbm, w2rows(0, z), local_sem.at[1]),
        pltpu.make_async_copy(dn_hbm, w2rows(1, z), local_sem.at[2]),
    ]
    locals_a = [
        pltpu.make_async_copy(r, qkv.at[i], local_sem.at[3 + i]) for i, r in enumerate((q_hbm, k_hbm, v_hbm))
    ]
    for d in locals_w + locals_a:
        d.start()

    bar = pltpu.get_barrier_semaphore()
    near = [{"tp": (t + j) % tp} for j in range(1, tp)]
    near += [{"sp": zz, "tp": 2 * x + cc} for zz in (zr, zl) for cc in (0, 1)]
    near += [{"groups": g + 1 - 2 * par}]
    for dev in near:
        pl.semaphore_signal(bar, inc=1, device_id=dev, device_id_type=MESH)
    pl.semaphore_wait(bar, len(near))

    hops = ((sp // 2 - 1, sp // 2), (sp // 2, sp // 2 - 1))

    def ring_ref(a, o):
        return wo_full.at[o] if a == 0 else w2rows(par, o)

    def ring_copy(a, d, k):
        o = (z - k + sp) % sp if d == 0 else (z + k) % sp
        return remote(
            ring_ref(a, o), ring_ref(a, o), ring_send.at[2 * a + d], ring_recv.at[2 * a + d, k],
            {"sp": zr if d == 0 else zl},
        )

    def ring_arrival(a, d, k):
        o = (z - 1 - k + 2 * sp) % sp if d == 0 else (z + 1 + k) % sp
        ref = ring_ref(a, o)
        return remote(ref, ref, ring_send.at[2 * a + d], ring_recv.at[2 * a + d, k], {"sp": zr if d == 0 else zl}), o

    def push(o):
        remote(w2rows(par, o), w2rows(par, o), pair_sem.at[0], pair_sem.at[1], {"groups": g + 1 - 2 * par}).start()

    def ring_step(a, k):
        for d in (0, 1):
            if k >= 1 and k - 1 < hops[a][d]:
                arrival, o = ring_arrival(a, d, k - 1)
                arrival.wait_recv()
                if a == 1:
                    push(o)
            if k < hops[a][d]:
                ring_copy(a, d, k).start()

    last = sp // 2
    done = [0, 0]

    def advance(n_wo=0, n_w2=0):
        for i in range(max(n_wo, n_w2)):
            for a, n in ((0, n_wo), (1, n_w2)):
                if i < n and done[a] <= last:
                    ring_step(a, done[a])
                    done[a] += 1

    for d in locals_w:
        d.wait()
    advance(1, 1)
    for d in locals_a:
        d.wait()

    slot = 2 * z + c

    def head_cols(h):
        return pl.ds(pl.multiple_of(h * feats, 128), feats)

    def send_heads(e):
        zz = (z + e + sp) % sp
        for m in (0, 1):
            remote(
                qkv.at[:, m, :, head_cols(zz)], qkvr.at[:, slot], a2a_sem.at[0], a2a_sem.at[1],
                {"sp": zz, "tp": 2 * x + m},
            ).start()

    def send_both(lo, hi):
        def one(e, carry):
            send_heads(e)
            send_heads(-e)
            return carry
        lax.fori_loop(lo, hi, one, 0)

    remote(
        qkv.at[:, 1 - c, :, head_cols(z)], qkvr.at[:, slot], a2a_sem.at[0], a2a_sem.at[1], {"tp": sib}
    ).start()
    qkvr[:, slot] = qkv[:, c, :, head_cols(z)]
    send_both(1, 2)
    reach, r = 1, 0
    while reach < sp // 2:
        for zz in ((z + reach) % sp, (z - reach + sp) % sp):
            pl.semaphore_signal(far_sem.at[r], inc=1, device_id={"sp": zz}, device_id_type=MESH)
        pl.semaphore_wait(far_sem.at[r], 2)
        send_both(reach + 1, min(2 * reach, sp // 2 - 1) + 1)
        reach, r = 2 * reach, r + 1
        advance(1, 0)
    send_heads(sp // 2)
    advance(0, 1)
    n = 2 * sp
    rest = qkvr.at[:, pl.ds(0, n - 1)]
    pltpu.make_async_copy(rest, rest, a2a_sem.at[1]).wait()

    own_kv = qkvr.at[pl.ds(1, 2)]
    right, left = {"tp": 2 * xr + c}, {"tp": 2 * xl + c}
    send(own_kv, kvo.at[0], kv_sem.at[0], kv_sem.at[4], right)
    send(own_kv, kvo.at[1], kv_sem.at[1], kv_sem.at[5], left)
    advance(1, 1)

    def pack(ref):
        v = ref[...].astype(F32)
        return v.reshape(v.shape[0] * v.shape[1], v.shape[2]).astype(BF16)

    rows = 8 * n
    qp[...] = pack(qkvr.at[0])
    kp[pl.ds(0, rows), :] = pack(qkvr.at[1])
    vp[pl.ds(0, rows), :] = pack(qkvr.at[2])
    remote(own_kv, kvo.at[0], kv_sem.at[0], kv_sem.at[4], right).wait_recv()
    send(kvo.at[0, 0], kvo.at[2, 0], kv_sem.at[2], kv_sem.at[6], right)
    remote(own_kv, kvo.at[1], kv_sem.at[1], kv_sem.at[5], left).wait_recv()
    send(kvo.at[1, 1], kvo.at[2, 1], kv_sem.at[3], kv_sem.at[7], left)
    for j in (0, 1):
        kp[pl.ds((1 + j) * rows, rows), :] = pack(kvo.at[j, 0])
        vp[pl.ds((1 + j) * rows, rows), :] = pack(kvo.at[j, 1])
    advance(1, 1)
    remote(kvo.at[0, 0], kvo.at[2, 0], kv_sem.at[2], kv_sem.at[6], right).wait_recv()
    remote(kvo.at[1, 1], kvo.at[2, 1], kv_sem.at[3], kv_sem.at[7], left).wait_recv()
    kp[pl.ds(3 * rows, rows), :] = pack(kvo.at[2, 0])
    vp[pl.ds(3 * rows, rows), :] = pack(kvo.at[2, 1])

    scale = 1.0 / math.sqrt(feats)
    qb = 128

    def attend(i, carry):
        q = qp[pl.ds(pl.multiple_of(i * qb, qb), qb), :]
        high = None
        for j in range(nx):
            s = dot_last(q, kp[j * rows : (j + 1) * rows, :])
            scores[:, j * rows : (j + 1) * rows] = s
            top = jnp.max(s, axis=1, keepdims=True)
            high = top if high is None else jnp.maximum(high, top)
        total = jnp.zeros((qb, 1), F32)
        acc = jnp.zeros((qb, feats), F32)
        for j in range(nx):
            e = jnp.exp((scores[:, j * rows : (j + 1) * rows] - high) * scale)
            total += jnp.sum(e, axis=1, keepdims=True)
            acc += dot(e.astype(BF16), vp[j * rows : (j + 1) * rows, :])
        o = acc / total
        att[pl.ds(i * (qb // 8), qb // 8)] = o.reshape(qb // 8, 8, feats).astype(BF16)
        return carry

    lax.fori_loop(0, rows // qb, attend, 0)
    advance(2, 1)

    def send_back(zz, cc):
        return remote(
            att.at[2 * zz + cc], att_all.at[c, 2 * x + cc, :, head_cols(z)], back_sem.at[0], back_sem.at[1],
            {"sp": zz, "tp": 2 * x + cc},
        )

    def back_one(e, carry):
        zz = (z + e) % sp
        send_back(zz, 0).start()
        send_back(zz, 1).start()
        return carry

    lax.fori_loop(1, sp, back_one, 0)
    remote(
        att.at[2 * z + 1 - c], att_all.at[c, sib, :, head_cols(z)], back_sem.at[0], back_sem.at[1], {"tp": sib}
    ).start()
    att_all[c, t, :, head_cols(z)] = att[slot]
    advance(4, 2)
    most = att.at[pl.ds(0, n - 1)]
    pltpu.make_async_copy(most, most, back_sem.at[1]).wait()

    def tp_gather(full, half, sems, between):
        rs = lambda i: sems.at[1, i]
        ss = lambda i: sems.at[0, i]
        tl, tr, to = 2 * xl + c, 2 * xr + c, 2 * xo + c
        sibling = {"tp": sib}

        def got(ref, i):
            remote(ref, ref, ss(i), rs(i), sibling).wait_recv()

        send(full(t), full(t), ss(0), rs(0), right)
        send(full(t), full(t), ss(1), rs(1), left)
        send(full(t), full(t), ss(2), rs(2), sibling)
        between()
        got(full(tl), 0)
        send(half(tl, 0), half(tl, 0), ss(3), rs(3), right)
        send(full(tl), full(tl), ss(4), rs(4), sibling)
        got(full(tr), 1)
        send(half(tr, 1), half(tr, 1), ss(5), rs(5), left)
        send(full(tr), full(tr), ss(6), rs(6), sibling)
        got(half(to, 0), 3)
        send(half(to, 0), half(to, 0), ss(7), rs(7), sibling)
        got(half(to, 1), 5)
        send(half(to, 1), half(to, 1), ss(8), rs(8), sibling)
        d = 1 - 2 * c
        got(full(t + d), 2)
        got(full(tl + d), 4)
        got(full(tr + d), 6)
        got(half(to + d, 0), 7)
        got(half(to + d, 1), 8)

    tp_gather(lambda i: att_all.at[:, i], lambda i, h: att_all.at[h, i], gat_sem, lambda: advance(2, 1))
    advance(sp, 0)

    nrow, width = mixed.shape
    mixed[...] = jnp.zeros_like(mixed)

    def project(i, carry):
        acc = jnp.zeros((nrow, width), F32)
        for u in range(4):
            h = i * 4 + u
            a = att_all[:, :, :, head_cols(h)].astype(F32).reshape(nrow, feats).astype(BF16)
            acc += dot_last(a, wo_full[h])
        mixed[...] += acc
        return carry

    lax.fori_loop(0, heads // 4, project, 0)
    res = res_ref[...].astype(F32).reshape(nrow, width)
    mix = res + mod_ref[0:1, :] * mixed[...]
    mixed[...] = mix
    local_sum = jnp.sum(mix, axis=1, keepdims=True)
    off = mix - local_sum * (1.0 / width)
    local_sq = jnp.sum(off * off, axis=1, keepdims=True)

    def as_row(col):
        return jnp.transpose(jnp.broadcast_to(col, (nrow, nrow)))[0:4, :]

    stats[t] = jnp.concatenate([as_row(local_sum), as_row(local_sq)], axis=0)
    advance(0, 1)
    for j in range(1, tp):
        dev = (t + j) % tp
        remote(stats.at[t], stats.at[t], st_sem.at[0], st_sem.at[1], {"tp": dev}).start()
    others = stats.at[pl.ds(0, tp - 1)]
    pltpu.make_async_copy(others, others, st_sem.at[1]).wait()
    every = stats[...]
    sums, squares = every[:, 0:1, :], every[:, 4:5, :]
    mean = jnp.sum(sums, axis=0) * (1.0 / (tp * width))
    shift = sums * (1.0 / width) - mean[None]
    spread = (jnp.sum(squares, axis=0) + width * jnp.sum(shift * shift, axis=0)) * (1.0 / (tp * width))
    inv = lax.rsqrt(spread + 1e-06)

    def as_col(row):
        return jnp.transpose(jnp.broadcast_to(row, (nrow, nrow)))[:, 0:1]

    mix = mixed[...]
    normed = (mix - as_col(mean)) * as_col(inv) * (1.0 + mod_ref[2:3, :]) + mod_ref[1:2, :]
    normed_all[t] = normed.astype(BF16)
    advance(0, 1)
    hr = nrow // 2
    tp_gather(
        lambda i: normed_all.at[i], lambda i, h: normed_all.at[i, pl.ds(h * hr, hr), :], gnm_sem, lambda: advance(0, 1)
    )
    advance(0, sp)
    pushed = w2.at[1 - par, pl.ds(0, (sp - 1) * shard), :]
    pltpu.make_async_copy(pushed, pushed, pair_sem.at[1]).wait()

    ff = active.shape[1]
    for lo in range(0, ff, 256):
        hi = min(lo + 256, ff)
        acc = jnp.zeros((nrow, hi - lo), F32)
        for i in range(tp):
            acc += dot(normed_all[i], w2[0, i * width : (i + 1) * width, lo:hi])
        inner = math.sqrt(2 / math.pi) * (acc + 0.044715 * (acc * acc * acc))
        active[:, lo:hi] = (0.5 * acc * (1.0 + jnp.tanh(inner))).astype(BF16)

    def down(i):
        dev = (t + i) % tp
        block = w2[1, pl.ds(pl.multiple_of(dev * width, 16), width), :]
        return dev, dot_last(active[...], block).astype(BF16)

    waiting = None
    for i in (4, 5, 3, 2, 6, 7, 1, 0):
        dev, block = down(i)
        if i:
            part_send[dev] = block
        else:
            part_recv[t] = block
        if waiting is not None:
            remote(part_send.at[waiting], part_recv.at[t], rs_sem.at[0], rs_sem.at[1], {"tp": waiting}).start()
        waiting = dev
    seven = part_recv.at[pl.ds(0, tp - 1)]
    pltpu.make_async_copy(seven, seven, rs_sem.at[1]).wait()
    total = part_recv[0].astype(F32)
    for i in range(1, tp):
        total += part_recv[i].astype(F32)
    out = mixed[...] + mod_ref[3:4, :] * total
    out_ref[...] = out.astype(BF16).reshape(out_ref.shape)

    for d in pending:
        d.wait_send()
    pltpu.make_async_copy(rest, rest, a2a_sem.at[0]).wait()
    pltpu.make_async_copy(most, most, back_sem.at[0]).wait()
    pltpu.make_async_copy(others, others, st_sem.at[0]).wait()
    pltpu.make_async_copy(seven, seven, rs_sem.at[0]).wait()
    pltpu.make_async_copy(pushed, pushed, pair_sem.at[0]).wait()
    for a in (0, 1):
        for d in (0, 1):
            k = hops[a][d]
            ref = wo_full.at[pl.ds(0, k)] if a == 0 else w2.at[par, pl.ds(0, k * shard), :]
            pltpu.make_async_copy(ref, ref, ring_send.at[2 * a + d]).wait()


def block(sp, tp, q, k, v, residual, modulation, wo, up, dn):
    mb, tokens, inner = q.shape
    feats = inner // sp
    width = wo.shape[0]
    nrow = mb * residual.shape[1]
    shard, ff = up.shape
    nslot = 2 * sp
    rows = tokens * nslot
    dma, reg = pltpu.SemaphoreType.DMA, pltpu.SemaphoreType.REGULAR
    anyspace = pl.BlockSpec(memory_space=pl.ANY)
    vmem = pl.BlockSpec(memory_space=pltpu.VMEM)
    V = pltpu.VMEM
    return pl.pallas_call(
        functools.partial(kernel, sp, tp),
        out_shape=jax.ShapeDtypeStruct(residual.shape, BF16),
        in_specs=[anyspace] * 3 + [vmem] * 2 + [anyspace] * 3,
        out_specs=vmem,
        scratch_shapes=[
            V((3, mb, tokens, inner), BF16),
            V((3, nslot, tokens, feats), BF16),
            V((3, 2, nslot, tokens, feats), BF16),
            V((rows, feats), BF16),
            V((tp // 2 * rows, feats), BF16),
            V((tp // 2 * rows, feats), BF16),
            V((128, tp // 2 * rows), F32),
            V((nslot, tokens, feats), BF16),
            V((mb, tp, tokens, inner), BF16),
            V((sp, width, feats), BF16),
            V((2, sp * shard, ff), BF16),
            V((nrow, width), F32),
            V((tp, 8, 128), F32),
            V((tp, nrow, width), BF16),
            V((nrow, ff), BF16),
            V((tp, nrow, width), BF16),
            V((tp, nrow, width), BF16),
            dma((6,)), dma((4, sp // 2)), dma((4,)), dma((2,)), reg((8,)), dma((2,)), dma((8,)), dma((2,)),
            dma((2, 9)), dma((2, 9)), dma((2,)), dma((2,)),
        ],
        compiler_params=pltpu.CompilerParams(
            collective_id=0, has_side_effects=True, vmem_limit_bytes=60 * 1024 * 1024
        ),
    )(q, k, v, residual, modulation, wo, up, dn)


def solution(mesh):
    in_specs = (
        P("groups", ("sp", "tp"), None),
        P("groups", ("sp", "tp"), None),
        P("groups", ("sp", "tp"), None),
        P("groups", "sp", "tp"),
        P(None, "tp"),
        P("tp", "sp"),
        P("sp", "tp"),
        P("sp", "tp"),
    )
    body = functools.partial(block, mesh.shape["sp"], mesh.shape["tp"])
    return jax.shard_map(body, mesh=mesh, in_specs=in_specs, out_specs=P("groups", "sp", "tp"), check_vma=False)
```

time: 619 us -> 238 us (0.38)
  waiting for transfers between devices: 322 us -> 0 us
  Pallas kernels: 0 us -> 237 us
  blocking collectives: 220 us -> 0 us
  local copies, waits for them, and re-layouts: 37.8 us -> 1.54 us
  between operations: 13.3 us -> 0.01 us
  matrix products: 11.6 us -> 0 us
  starting transfers between devices: 10.3 us -> 0 us
    all_gather x4 -> x0, waiting for transfers between devices: 305 us -> none  [the longest x1 135 us: body(): lax.all_gather(up_weight, 'sp', axis=0, tiled=True)]
    pallas_call x0 -> x1, Pallas kernels: none -> 237 us  [block(): pl.pallas_call(functools.partial(kernel, sp, tp), out_shape=jax.ShapeDtyp...]
    all_to_all x4 -> x0, blocking collectives: 220 us -> none  [the longest x1 97.4 us: in_one_piece(): lax.all_to_all(both, axis, split_axis=split_dim, concat_axis=concat_dim,...]
    unnamed x6 -> x1, local copies, waits for them, and re-layouts: 17.9 us -> 1.54 us
    all_to_all x2 -> x0, waiting for transfers between devices: 14.9 us -> none  [sent_to_all(): return lax.all_to_all(copies, axis, split_axis=0, concat_axis=0, tiled=True)]
    dot_general x10 -> x0, matrix products: 11.6 us -> none  [the longest x2 8.65 us: contract_last(): lax.dot_general(left, right, (((1,), (1,)), ((), ())), preferred_element_...]
    all_to_all x2 -> x0, starting transfers between devices: 10.1 us -> none  [sent_to_all(): return lax.all_to_all(copies, axis, split_axis=0, concat_axis=0, tiled=True)]
    all_to_all x3 -> x0, local copies, waits for them, and re-layouts: 7.49 us -> none  [the longest x1 7.38 us: in_one_piece(): lax.all_to_all(both, axis, split_axis=split_dim, concat_axis=concat_dim,...]
  transfers between devices with their start and end apart: 6 -> 0, of which waited for: 5 -> 0; matrix products, arithmetic and copies ran while one was open for 2% -> 0% of each run, Pallas kernels for 0% -> 0%
where the time goes in v1:
time: 238 us
  Pallas kernels  237 us (100%)
    pallas_call x1, Pallas kernels, block(): pl.pallas_call(functools.partial(kernel, sp, tp), out_shape=jax.ShapeDtyp...  237 us

profile of v1, /device:TPU:33, one launch (start us, length us, event | category | flops | bytes accessed | tf_op | source)
XLA Modules:
  0.0 238.2 jit_solution(12920997534481909024)
XLA Ops:
  0.0 236.7 %shard_map.82 = bf16[2,64,320]{2,1,0:T(8,128)(2,1)} custom-call(bf16[2,8,4096]{2,1,0:T(8,128)(2,1)} %q_hbm.1, bf16[2,8,4096]{2,1,0:T(8,128)(2,1)} %k_hbm.1, bf16[2,8,4096]{2,1,0:T(8,128)(2,1)} %v_hbm.1, bf16[2,64,320]{2,1,0:T(8,128)(2,1)} %res_ref.1, f32[4,320]{1,0:T(4,128)} %mod_ref.1, bf16[320,128]{1,0:T(8,128)(2,1)} %wo_hbm.1, bf16[80,896]{1,0:T(8,128)(2,1)} %up_hbm.1, ...), custom_call_target="tpu_custom_call" | custom-call | tf_op jit(solution)/shard_map/pallas_call | solution.py:374
  236.7 1.5 copy.10

commit v2 on v1

--- a/solution.py
+++ b/solution.py
@@ -25,7 +25,7 @@
     sp, tp, q_hbm, k_hbm, v_hbm, res_ref, mod_ref, wo_hbm, up_hbm, dn_hbm, out_ref,
     qkv, qkvr, kvo, qp, kp, vp, scores, att, att_all, wo_full, w2, mixed, stats, normed_all,
     active, part_send, part_recv,
-    local_sem, ring_recv, ring_send, pair_sem, far_sem, a2a_sem, kv_sem, back_sem, gat_sem, gnm_sem, st_sem, rs_sem,
+    local_sem, ring_recv, ring_send, pair_sem, below_sem, hello_sem, a2a_sem, kv_sem, back_sem, gat_sem, gnm_sem, st_sem, rs_sem,
 ):
     heads, feats = sp, qkvr.shape[-1]
     nx = tp // 2
@@ -64,12 +64,28 @@
         d.start()
 
     bar = pltpu.get_barrier_semaphore()
-    near = [{"tp": (t + j) % tp} for j in range(1, tp)]
-    near += [{"sp": zz, "tp": 2 * x + cc} for zz in (zr, zl) for cc in (0, 1)]
-    near += [{"groups": g + 1 - 2 * par}]
-    for dev in near:
-        pl.semaphore_signal(bar, inc=1, device_id=dev, device_id_type=MESH)
-    pl.semaphore_wait(bar, len(near))
+    beside = [{"tp": (t + j) % tp} for j in range(1, tp)] + [{"groups": g + 1 - 2 * par}]
+
+    def greet(devs):
+        for dev in devs:
+            pl.semaphore_signal(bar, inc=1, device_id=dev, device_id_type=MESH)
+
+    greet(beside)
+    pl.when(z > 0)(lambda: greet([{"sp": zl, "tp": 2 * x + cc} for cc in (0, 1)]))
+    pl.when(z < sp - 1)(lambda: greet([{"sp": zr, "tp": 2 * x + cc} for cc in (0, 1)]))
+    pl.semaphore_wait(bar, len(beside) + 2 * jnp.minimum(z, 1) + 2 * jnp.minimum(sp - 1 - z, 1))
+
+    pl.when(z > 0)(lambda: pl.semaphore_wait(below_sem.at[0], 1))
+
+    @pl.when(z < sp - 1)
+    def _():
+        pl.semaphore_signal(below_sem.at[0], inc=1, device_id={"sp": zr}, device_id_type=MESH)
+
+    def hello(zz, carry):
+        pl.semaphore_signal(hello_sem.at[z], inc=1, device_id={"sp": zz}, device_id_type=MESH)
+        return carry
+
+    lax.fori_loop(0, z, hello, 0)
 
     hops = ((sp // 2 - 1, sp // 2), (sp // 2, sp // 2 - 1))
 
@@ -91,29 +107,42 @@
     def push(o):
         remote(w2rows(par, o), w2rows(par, o), pair_sem.at[0], pair_sem.at[1], {"groups": g + 1 - 2 * par}).start()
 
-    def ring_step(a, k):
+    def ring_part(a, k):
         for d in (0, 1):
-            if k >= 1 and k - 1 < hops[a][d]:
+            @pl.when(k - 1 < hops[a][d])
+            def _():
                 arrival, o = ring_arrival(a, d, k - 1)
                 arrival.wait_recv()
                 if a == 1:
                     push(o)
-            if k < hops[a][d]:
+
+            @pl.when(k < hops[a][d])
+            def _():
                 ring_copy(a, d, k).start()
 
-    last = sp // 2
-    done = [0, 0]
-
-    def advance(n_wo=0, n_w2=0):
-        for i in range(max(n_wo, n_w2)):
-            for a, n in ((0, n_wo), (1, n_w2)):
-                if i < n and done[a] <= last:
-                    ring_step(a, done[a])
-                    done[a] += 1
+    half = sp // 2
+
+    def ring_step(i, carry):
+        pl.when(i <= half)(lambda: ring_part(0, i))
+        pl.when((i > half) | (i % 2 == 0))(lambda: ring_part(1, jnp.where(i > half, i - half // 2, i // 2)))
+        return carry
+
+    last = half + half // 2
+    at = [None]
+
+    def advance(n=1, upto=0):
+        end = jnp.minimum(jnp.maximum(at[0] + n, upto), last + 1)
+        lax.fori_loop(at[0], end, ring_step, 0)
+        at[0] = end
+
+    def ring_start(d):
+        ring_copy(0, d, 0).start()
+        ring_copy(1, d, 0).start()
 
     for d in locals_w:
         d.wait()
-    advance(1, 1)
+    ring_start(0)
+    pl.when(z > 0)(lambda: ring_start(1))
     for d in locals_a:
         d.wait()
 
@@ -130,28 +159,30 @@
                 {"sp": zz, "tp": 2 * x + m},
             ).start()
 
-    def send_both(lo, hi):
-        def one(e, carry):
-            send_heads(e)
-            send_heads(-e)
-            return carry
-        lax.fori_loop(lo, hi, one, 0)
-
     remote(
         qkv.at[:, 1 - c, :, head_cols(z)], qkvr.at[:, slot], a2a_sem.at[0], a2a_sem.at[1], {"tp": sib}
     ).start()
     qkvr[:, slot] = qkv[:, c, :, head_cols(z)]
-    send_both(1, 2)
-    reach, r = 1, 0
-    while reach < sp // 2:
-        for zz in ((z + reach) % sp, (z - reach + sp) % sp):
-            pl.semaphore_signal(far_sem.at[r], inc=1, device_id={"sp": zz}, device_id_type=MESH)
-        pl.semaphore_wait(far_sem.at[r], 2)
-        send_both(reach + 1, min(2 * reach, sp // 2 - 1) + 1)
-        reach, r = 2 * reach, r + 1
-        advance(1, 0)
-    send_heads(sp // 2)
-    advance(0, 1)
+
+    def down_one(e, carry):
+        send_heads(-e)
+        return carry
+
+    def up_one(e, carry):
+        pl.semaphore_wait(hello_sem.at[z + e], 1)
+        send_heads(e)
+
+        @pl.when((e % 2 == 0) & (e // 2 <= z))
+        def _():
+            ring_step(e // 2, 0)
+
+        return carry
+
+    lax.fori_loop(1, z + 1, down_one, 0)
+    lax.fori_loop(1, sp - z, up_one, 0)
+    pl.when(z == 0)(lambda: ring_start(1))
+    at[0] = 1 + jnp.minimum((sp - 1 - z) // 2, z)
+    advance(1)
     n = 2 * sp
     rest = qkvr.at[:, pl.ds(0, n - 1)]
     pltpu.make_async_copy(rest, rest, a2a_sem.at[1]).wait()
@@ -160,7 +191,7 @@
     right, left = {"tp": 2 * xr + c}, {"tp": 2 * xl + c}
     send(own_kv, kvo.at[0], kv_sem.at[0], kv_sem.at[4], right)
     send(own_kv, kvo.at[1], kv_sem.at[1], kv_sem.at[5], left)
-    advance(1, 1)
+    advance(2)
 
     def pack(ref):
         v = ref[...].astype(F32)
@@ -177,7 +208,7 @@
     for j in (0, 1):
         kp[pl.ds((1 + j) * rows, rows), :] = pack(kvo.at[j, 0])
         vp[pl.ds((1 + j) * rows, rows), :] = pack(kvo.at[j, 1])
-    advance(1, 1)
+    advance(2)
     remote(kvo.at[0, 0], kvo.at[2, 0], kv_sem.at[2], kv_sem.at[6], right).wait_recv()
     remote(kvo.at[1, 1], kvo.at[2, 1], kv_sem.at[3], kv_sem.at[7], left).wait_recv()
     kp[pl.ds(3 * rows, rows), :] = pack(kvo.at[2, 0])
@@ -205,7 +236,7 @@
         return carry
 
     lax.fori_loop(0, rows // qb, attend, 0)
-    advance(2, 1)
+    advance(2)
 
     def send_back(zz, cc):
         return remote(
@@ -224,7 +255,7 @@
         att.at[2 * z + 1 - c], att_all.at[c, sib, :, head_cols(z)], back_sem.at[0], back_sem.at[1], {"tp": sib}
     ).start()
     att_all[c, t, :, head_cols(z)] = att[slot]
-    advance(4, 2)
+    advance(5)
     most = att.at[pl.ds(0, n - 1)]
     pltpu.make_async_copy(most, most, back_sem.at[1]).wait()
 
@@ -258,8 +289,8 @@
         got(half(to + d, 0), 7)
         got(half(to + d, 1), 8)
 
-    tp_gather(lambda i: att_all.at[:, i], lambda i, h: att_all.at[h, i], gat_sem, lambda: advance(2, 1))
-    advance(sp, 0)
+    tp_gather(lambda i: att_all.at[:, i], lambda i, h: att_all.at[h, i], gat_sem, lambda: advance(2))
+    advance(0, half + 1)
 
     nrow, width = mixed.shape
     mixed[...] = jnp.zeros_like(mixed)
@@ -285,7 +316,7 @@
         return jnp.transpose(jnp.broadcast_to(col, (nrow, nrow)))[0:4, :]
 
     stats[t] = jnp.concatenate([as_row(local_sum), as_row(local_sq)], axis=0)
-    advance(0, 1)
+    advance(1)
     for j in range(1, tp):
         dev = (t + j) % tp
         remote(stats.at[t], stats.at[t], st_sem.at[0], st_sem.at[1], {"tp": dev}).start()
@@ -304,12 +335,12 @@
     mix = mixed[...]
     normed = (mix - as_col(mean)) * as_col(inv) * (1.0 + mod_ref[2:3, :]) + mod_ref[1:2, :]
     normed_all[t] = normed.astype(BF16)
-    advance(0, 1)
+    advance(1)
     hr = nrow // 2
     tp_gather(
-        lambda i: normed_all.at[i], lambda i, h: normed_all.at[i, pl.ds(h * hr, hr), :], gnm_sem, lambda: advance(0, 1)
+        lambda i: normed_all.at[i], lambda i, h: normed_all.at[i, pl.ds(h * hr, hr), :], gnm_sem, lambda: advance(1)
     )
-    advance(0, sp)
+    advance(sp)
     pushed = w2.at[1 - par, pl.ds(0, (sp - 1) * shard), :]
     pltpu.make_async_copy(pushed, pushed, pair_sem.at[1]).wait()
 
@@ -394,7 +425,7 @@
             V((nrow, ff), BF16),
             V((tp, nrow, width), BF16),
             V((tp, nrow, width), BF16),
-            dma((6,)), dma((4, sp // 2)), dma((4,)), dma((2,)), reg((8,)), dma((2,)), dma((8,)), dma((2,)),
+            dma((6,)), dma((4, sp // 2)), dma((4,)), dma((2,)), reg((1,)), reg((sp,)), dma((2,)), dma((8,)), dma((2,)),
             dma((2, 9)), dma((2, 9)), dma((2,)), dma((2,)),
         ],
         compiler_params=pltpu.CompilerParams(

time: 238 us -> 317 us (1.33)
  the two profiles are of different devices: /device:TPU:33 before, /device:TPU:104 now
where the time goes in v2:
time: 317 us; the launch traced here: 316 us
  Pallas kernels  315 us (99%)
    pallas_call x1, Pallas kernels, block(): pl.pallas_call(functools.partial(kernel, sp, tp), out_shape=jax.ShapeDtyp...  315 us

profile of v2, /device:TPU:104, one launch (start us, length us, event | category | flops | bytes accessed | tf_op | source)
XLA Modules:
  0.0 316.3 jit_solution(10212728314923069529)
XLA Ops:
  0.0 314.7 %shard_map.82 = bf16[2,64,320]{2,1,0:T(8,128)(2,1)} custom-call(bf16[2,8,4096]{2,1,0:T(8,128)(2,1)} %q_hbm.1, bf16[2,8,4096]{2,1,0:T(8,128)(2,1)} %k_hbm.1, bf16[2,8,4096]{2,1,0:T(8,128)(2,1)} %v_hbm.1, bf16[2,64,320]{2,1,0:T(8,128)(2,1)} %res_ref.1, f32[4,320]{1,0:T(4,128)} %mod_ref.1, bf16[320,128]{1,0:T(8,128)(2,1)} %wo_hbm.1, bf16[80,896]{1,0:T(8,128)(2,1)} %up_hbm.1, ...), custom_call_target="tpu_custom_call" | custom-call | tf_op jit(solution)/shard_map/pallas_call | solution.py:405
  314.8 1.5 copy.10

commit v3 on v1

--- a/solution.py
+++ b/solution.py
@@ -149,9 +149,10 @@
         pl.semaphore_wait(far_sem.at[r], 2)
         send_both(reach + 1, min(2 * reach, sp // 2 - 1) + 1)
         reach, r = 2 * reach, r + 1
-        advance(1, 0)
+        if r < 4:
+            advance(1, 1)
     send_heads(sp // 2)
-    advance(0, 1)
+    advance(0, 4)
     n = 2 * sp
     rest = qkvr.at[:, pl.ds(0, n - 1)]
     pltpu.make_async_copy(rest, rest, a2a_sem.at[1]).wait()
@@ -172,6 +173,7 @@
     vp[pl.ds(0, rows), :] = pack(qkvr.at[2])
     remote(own_kv, kvo.at[0], kv_sem.at[0], kv_sem.at[4], right).wait_recv()
     send(kvo.at[0, 0], kvo.at[2, 0], kv_sem.at[2], kv_sem.at[6], right)
+    advance(1, 1)
     remote(own_kv, kvo.at[1], kv_sem.at[1], kv_sem.at[5], left).wait_recv()
     send(kvo.at[1, 1], kvo.at[2, 1], kv_sem.at[3], kv_sem.at[7], left)
     for j in (0, 1):
@@ -205,7 +207,7 @@
         return carry
 
     lax.fori_loop(0, rows // qb, attend, 0)
-    advance(2, 1)
+    advance(1, 1)
 
     def send_back(zz, cc):
         return remote(
@@ -224,7 +226,7 @@
         att.at[2 * z + 1 - c], att_all.at[c, sib, :, head_cols(z)], back_sem.at[0], back_sem.at[1], {"tp": sib}
     ).start()
     att_all[c, t, :, head_cols(z)] = att[slot]
-    advance(4, 2)
+    advance(2, 2)
     most = att.at[pl.ds(0, n - 1)]
     pltpu.make_async_copy(most, most, back_sem.at[1]).wait()
 
@@ -247,6 +249,7 @@
         got(full(tr), 1)
         send(half(tr, 1), half(tr, 1), ss(5), rs(5), left)
         send(full(tr), full(tr), ss(6), rs(6), sibling)
+        between()
         got(half(to, 0), 3)
         send(half(to, 0), half(to, 0), ss(7), rs(7), sibling)
         got(half(to, 1), 5)
@@ -258,7 +261,7 @@
         got(half(to + d, 0), 7)
         got(half(to + d, 1), 8)
 
-    tp_gather(lambda i: att_all.at[:, i], lambda i, h: att_all.at[h, i], gat_sem, lambda: advance(2, 1))
+    tp_gather(lambda i: att_all.at[:, i], lambda i, h: att_all.at[h, i], gat_sem, lambda: advance(3, 1))
     advance(sp, 0)
 
     nrow, width = mixed.shape

time: 238 us -> 214 us (0.90)
  Pallas kernels: 237 us -> 212 us
    pallas_call x1, Pallas kernels: 237 us -> 212 us  [block(): pl.pallas_call(functools.partial(kernel, sp, tp), out_shape=jax.ShapeDtyp...]
where the time goes in v3:
time: 214 us
  Pallas kernels  212 us (99%)
    pallas_call x1, Pallas kernels, block(): pl.pallas_call(functools.partial(kernel, sp, tp), out_shape=jax.ShapeDtyp...  212 us

profile of v3, /device:TPU:33, one launch (start us, length us, event | category | flops | bytes accessed | tf_op | source)
XLA Modules:
  0.0 214.0 jit_solution(10114677739853483930)
XLA Ops:
  0.0 212.4 %shard_map.82 = bf16[2,64,320]{2,1,0:T(8,128)(2,1)} custom-call(bf16[2,8,4096]{2,1,0:T(8,128)(2,1)} %q_hbm.1, bf16[2,8,4096]{2,1,0:T(8,128)(2,1)} %k_hbm.1, bf16[2,8,4096]{2,1,0:T(8,128)(2,1)} %v_hbm.1, bf16[2,64,320]{2,1,0:T(8,128)(2,1)} %res_ref.1, f32[4,320]{1,0:T(4,128)} %mod_ref.1, bf16[320,128]{1,0:T(8,128)(2,1)} %wo_hbm.1, bf16[80,896]{1,0:T(8,128)(2,1)} %up_hbm.1, ...), custom_call_target="tpu_custom_call" | custom-call | tf_op jit(solution)/shard_map/pallas_call | solution.py:377
  212.4 1.5 copy.10

commit v4 on v3

--- a/solution.py
+++ b/solution.py
@@ -24,8 +24,8 @@
 def kernel(
     sp, tp, q_hbm, k_hbm, v_hbm, res_ref, mod_ref, wo_hbm, up_hbm, dn_hbm, out_ref,
     qkv, qkvr, kvo, qp, kp, vp, scores, att, att_all, wo_full, w2, mixed, stats, normed_all,
-    active, part_send, part_recv,
-    local_sem, ring_recv, ring_send, pair_sem, far_sem, a2a_sem, kv_sem, back_sem, gat_sem, gnm_sem, st_sem, rs_sem,
+    active, part_send, part_out, sib_recv, part_recv,
+    local_sem, ring_recv, ring_send, pair_sem, far_sem, a2a_sem, kv_sem, back_sem, gat_sem, gnm_sem, st_sem, rs_sem, sib_sem,
 ):
     heads, feats = sp, qkvr.shape[-1]
     nx = tp // 2
@@ -73,8 +73,12 @@
 
     hops = ((sp // 2 - 1, sp // 2), (sp // 2, sp // 2 - 1))
 
+    quarter = wo_hbm.shape[0] // 4
+
     def ring_ref(a, o):
-        return wo_full.at[o] if a == 0 else w2rows(par, o)
+        if a == 0:
+            return wo_full.at[o, pl.ds(pl.multiple_of(par * quarter, 16), 3 * quarter), :]
+        return w2rows(par, o)
 
     def ring_copy(a, d, k):
         o = (z - k + sp) % sp if d == 0 else (z + k) % sp
@@ -88,16 +92,16 @@
         ref = ring_ref(a, o)
         return remote(ref, ref, ring_send.at[2 * a + d], ring_recv.at[2 * a + d, k], {"sp": zr if d == 0 else zl}), o
 
-    def push(o):
-        remote(w2rows(par, o), w2rows(par, o), pair_sem.at[0], pair_sem.at[1], {"groups": g + 1 - 2 * par}).start()
+    def push(a, o):
+        ref = wo_full.at[o, pl.ds(pl.multiple_of(par * 3 * quarter, 16), quarter), :] if a == 0 else w2rows(par, o)
+        remote(ref, ref, pair_sem.at[a, 0], pair_sem.at[a, 1], {"groups": g + 1 - 2 * par}).start()
 
     def ring_step(a, k):
         for d in (0, 1):
             if k >= 1 and k - 1 < hops[a][d]:
                 arrival, o = ring_arrival(a, d, k - 1)
                 arrival.wait_recv()
-                if a == 1:
-                    push(o)
+                push(a, o)
             if k < hops[a][d]:
                 ring_copy(a, d, k).start()
 
@@ -131,11 +135,12 @@
             ).start()
 
     def send_both(lo, hi):
-        def one(e, carry):
+        def one(i, carry):
+            e = hi - 1 - i
             send_heads(e)
             send_heads(-e)
             return carry
-        lax.fori_loop(lo, hi, one, 0)
+        lax.fori_loop(0, hi - lo, one, 0)
 
     remote(
         qkv.at[:, 1 - c, :, head_cols(z)], qkvr.at[:, slot], a2a_sem.at[0], a2a_sem.at[1], {"tp": sib}
@@ -147,12 +152,13 @@
         for zz in ((z + reach) % sp, (z - reach + sp) % sp):
             pl.semaphore_signal(far_sem.at[r], inc=1, device_id={"sp": zz}, device_id_type=MESH)
         pl.semaphore_wait(far_sem.at[r], 2)
+        if 2 * reach == sp // 2:
+            send_heads(sp // 2)
         send_both(reach + 1, min(2 * reach, sp // 2 - 1) + 1)
         reach, r = 2 * reach, r + 1
         if r < 4:
             advance(1, 1)
-    send_heads(sp // 2)
-    advance(0, 4)
+    advance(0, 2)
     n = 2 * sp
     rest = qkvr.at[:, pl.ds(0, n - 1)]
     pltpu.make_async_copy(rest, rest, a2a_sem.at[1]).wait()
@@ -207,7 +213,6 @@
         return carry
 
     lax.fori_loop(0, rows // qb, attend, 0)
-    advance(1, 1)
 
     def send_back(zz, cc):
         return remote(
@@ -215,18 +220,21 @@
             {"sp": zz, "tp": 2 * x + cc},
         )
 
-    def back_one(e, carry):
-        zz = (z + e) % sp
-        send_back(zz, 0).start()
-        send_back(zz, 1).start()
+    def back_one(i, carry):
+        for zz in ((z + half - i) % sp, (z + half + i) % sp):
+            send_back(zz, 0).start()
+            send_back(zz, 1).start()
         return carry
 
-    lax.fori_loop(1, sp, back_one, 0)
+    half = sp // 2
+    send_back((z + half) % sp, 0).start()
+    send_back((z + half) % sp, 1).start()
+    lax.fori_loop(1, half, back_one, 0)
     remote(
         att.at[2 * z + 1 - c], att_all.at[c, sib, :, head_cols(z)], back_sem.at[0], back_sem.at[1], {"tp": sib}
     ).start()
     att_all[c, t, :, head_cols(z)] = att[slot]
-    advance(2, 2)
+    advance(3, 3)
     most = att.at[pl.ds(0, n - 1)]
     pltpu.make_async_copy(most, most, back_sem.at[1]).wait()
 
@@ -263,6 +271,8 @@
 
     tp_gather(lambda i: att_all.at[:, i], lambda i, h: att_all.at[h, i], gat_sem, lambda: advance(3, 1))
     advance(sp, 0)
+    pushed_wo = wo_full.at[pl.ds(0, sp - 1), pl.ds(0, quarter), :]
+    pltpu.make_async_copy(pushed_wo, pushed_wo, pair_sem.at[0, 1]).wait()
 
     nrow, width = mixed.shape
     mixed[...] = jnp.zeros_like(mixed)
@@ -314,7 +324,7 @@
     )
     advance(0, sp)
     pushed = w2.at[1 - par, pl.ds(0, (sp - 1) * shard), :]
-    pltpu.make_async_copy(pushed, pushed, pair_sem.at[1]).wait()
+    pltpu.make_async_copy(pushed, pushed, pair_sem.at[1, 1]).wait()
 
     ff = active.shape[1]
     for lo in range(0, ff, 256):
@@ -325,25 +335,27 @@
         inner = math.sqrt(2 / math.pi) * (acc + 0.044715 * (acc * acc * acc))
         active[:, lo:hi] = (0.5 * acc * (1.0 + jnp.tanh(inner))).astype(BF16)
 
-    def down(i):
-        dev = (t + i) % tp
-        block = w2[1, pl.ds(pl.multiple_of(dev * width, 16), width), :]
-        return dev, dot_last(active[...], block).astype(BF16)
-
-    waiting = None
-    for i in (4, 5, 3, 2, 6, 7, 1, 0):
-        dev, block = down(i)
+    def down(tgt):
+        return dot_last(active[...], w2[1, pl.ds(pl.multiple_of(tgt * width, 16), width), :])
+
+    order = (xo, xr, xl, x)
+    to_sib = [remote(part_send.at[i], sib_recv.at[i], sib_sem.at[0, i], sib_sem.at[1, i], {"tp": sib}) for i in range(4)]
+    for i, xx in enumerate(order):
+        part_send[i] = down(2 * xx + 1 - c).astype(BF16)
         if i:
-            part_send[dev] = block
-        else:
-            part_recv[t] = block
-        if waiting is not None:
-            remote(part_send.at[waiting], part_recv.at[t], rs_sem.at[0], rs_sem.at[1], {"tp": waiting}).start()
-        waiting = dev
-    seven = part_recv.at[pl.ds(0, tp - 1)]
-    pltpu.make_async_copy(seven, seven, rs_sem.at[1]).wait()
-    total = part_recv[0].astype(F32)
-    for i in range(1, tp):
+            to_sib[i - 1].start()
+    total = down(2 * xo + c)
+    to_sib[3].start()
+    for i, seat in ((0, 0), (1, 2), (2, 1)):
+        to_sib[i].wait_recv()
+        part_out[i] = (total + sib_recv[i].astype(F32)).astype(BF16)
+        total = down(2 * order[i + 1] + c)
+        remote(part_out.at[i], part_recv.at[seat], rs_sem.at[0], rs_sem.at[1], {"tp": 2 * order[i] + c}).start()
+    to_sib[3].wait_recv()
+    total += sib_recv[3].astype(F32)
+    three = part_recv.at[pl.ds(0, 3)]
+    pltpu.make_async_copy(three, three, rs_sem.at[1]).wait()
+    for i in range(3):
         total += part_recv[i].astype(F32)
     out = mixed[...] + mod_ref[3:4, :] * total
     out_ref[...] = out.astype(BF16).reshape(out_ref.shape)
@@ -353,12 +365,15 @@
     pltpu.make_async_copy(rest, rest, a2a_sem.at[0]).wait()
     pltpu.make_async_copy(most, most, back_sem.at[0]).wait()
     pltpu.make_async_copy(others, others, st_sem.at[0]).wait()
-    pltpu.make_async_copy(seven, seven, rs_sem.at[0]).wait()
-    pltpu.make_async_copy(pushed, pushed, pair_sem.at[0]).wait()
+    pltpu.make_async_copy(three, three, rs_sem.at[0]).wait()
+    for d in to_sib:
+        d.wait_send()
+    pltpu.make_async_copy(pushed, pushed, pair_sem.at[1, 0]).wait()
+    pltpu.make_async_copy(pushed_wo, pushed_wo, pair_sem.at[0, 0]).wait()
     for a in (0, 1):
         for d in (0, 1):
             k = hops[a][d]
-            ref = wo_full.at[pl.ds(0, k)] if a == 0 else w2.at[par, pl.ds(0, k * shard), :]
+            ref = wo_full.at[pl.ds(0, k), pl.ds(0, 3 * quarter), :] if a == 0 else w2.at[par, pl.ds(0, k * shard), :]
             pltpu.make_async_copy(ref, ref, ring_send.at[2 * a + d]).wait()
 
 
@@ -395,10 +410,12 @@
             V((tp, 8, 128), F32),
             V((tp, nrow, width), BF16),
             V((nrow, ff), BF16),
-            V((tp, nrow, width), BF16),
-            V((tp, nrow, width), BF16),
-            dma((6,)), dma((4, sp // 2)), dma((4,)), dma((2,)), reg((8,)), dma((2,)), dma((8,)), dma((2,)),
-            dma((2, 9)), dma((2, 9)), dma((2,)), dma((2,)),
+            V((4, nrow, width), BF16),
+            V((3, nrow, width), BF16),
+            V((4, nrow, width), BF16),
+            V((3, nrow, width), BF16),
+            dma((6,)), dma((4, sp // 2)), dma((4,)), dma((2, 2)), reg((8,)), dma((2,)), dma((8,)), dma((2,)),
+            dma((2, 9)), dma((2, 9)), dma((2,)), dma((2,)), dma((2, 4)),
         ],
         compiler_params=pltpu.CompilerParams(
             collective_id=0, has_side_effects=True, vmem_limit_bytes=60 * 1024 * 1024

time: 214 us -> 206 us (0.963)
  Pallas kernels: 212 us -> 204 us
    pallas_call x1, Pallas kernels: 212 us -> 204 us  [block(): pl.pallas_call(functools.partial(kernel, sp, tp), out_shape=jax.ShapeDtyp...]
where the time goes in v4:
time: 206 us
  Pallas kernels  204 us (99%)
    pallas_call x1, Pallas kernels, block(): pl.pallas_call(functools.partial(kernel, sp, tp), out_shape=jax.ShapeDtyp...  204 us

profile of v4, /device:TPU:33, one launch (start us, length us, event | category | flops | bytes accessed | tf_op | source)
XLA Modules:
  0.0 205.8 jit_solution(3655759837013608820)
XLA Ops:
  0.0 204.3 %shard_map.82 = bf16[2,64,320]{2,1,0:T(8,128)(2,1)} custom-call(bf16[2,8,4096]{2,1,0:T(8,128)(2,1)} %q_hbm.1, bf16[2,8,4096]{2,1,0:T(8,128)(2,1)} %k_hbm.1, bf16[2,8,4096]{2,1,0:T(8,128)(2,1)} %v_hbm.1, bf16[2,64,320]{2,1,0:T(8,128)(2,1)} %res_ref.1, f32[4,320]{1,0:T(4,128)} %mod_ref.1, bf16[320,128]{1,0:T(8,128)(2,1)} %wo_hbm.1, bf16[80,896]{1,0:T(8,128)(2,1)} %up_hbm.1, ...), custom_call_target="tpu_custom_call" | custom-call | tf_op jit(solution)/shard_map/pallas_call | solution.py:392
  204.3 1.5 copy.10
